TPU v7x, 32 devices: a whole 2x2x4 slice. The times are simulated.
32 devices in a mesh: gx: 2 (over x), gy: 4 (over z), band: 4 (over y, core).
Axes of the slice: x: 2, y: 2, z: 4, core: 2. Of those that a mesh axis runs over, the one named last changes fastest.
Arguments:
- orbitals: float32 [2, 16, 16, 48, 128], P(None, 'band', 'gx', 'gy'), may hold values from -3 to 3
- external: float32 [16, 48, 128], P('gx', 'gy'), may hold values from 2 to 6
Outputs:
- orbitals_next: float32 [2, 16, 16, 48, 128], P(None, 'band', 'gx', 'gy')
- potential_next: float32 [16, 48, 128], P('gx', 'gy')
All inputs are finite; a program needn't handle non-finite values.
Results may differ from a plain program's by a relative error of at most 0.00002.
Values sent between devices are 32-bit elements; how exact they have to be, the bound alone decides.
A program may use at most 64 MiB of HBM per device.

v0:
```python
import jax
import jax.numpy as jnp
from jax import lax
from jax.sharding import PartitionSpec as P

step_length = 0.15
exchange_coef = 0.7386
centre_weight = -2.5
near_weight = 4.0 / 3.0
far_weight = -1.0 / 12.0


def with_halo(cells, sides, width):
    for axis, dim in sides:
        count = lax.axis_size(axis)
        ends = count - 1
        head = lax.slice_in_dim(cells, 0, width, axis=dim)
        tail = lax.slice_in_dim(cells, cells.shape[dim] - width, cells.shape[dim], axis=dim)
        cells = jnp.concatenate(
            [
                lax.ppermute(tail, axis, [(i, (i + 1) % count) for i in range(ends)]),
                cells,
                lax.ppermute(head, axis, [((i + 1) % count, i) for i in range(ends)]),
            ],
            axis=dim,
        )
    return cells


def shifted(padded, which_axis, offset):
    dimensions = padded.ndim
    selector = []
    for position in range(dimensions):
        if position < dimensions - 3:
            selector.append(slice(None))
        elif position == which_axis:
            selector.append(slice(2 + offset, padded.shape[position] - 2 + offset))
        else:
            selector.append(slice(2, padded.shape[position] - 2))
    return padded[tuple(selector)]


def laplacian(padded):
    dimensions = padded.ndim
    centre = shifted(padded, dimensions - 1, 0)
    summed = 3.0 * centre_weight * centre
    for which_axis in range(dimensions - 3, dimensions):
        summed = summed + near_weight * (
            shifted(padded, which_axis, 1) + shifted(padded, which_axis, -1)
        )
        summed = summed + far_weight * (
            shifted(padded, which_axis, 2) + shifted(padded, which_axis, -2)
        )
    return summed


def taylor(values, apply_fn, interval):
    summed = values
    taylor_term = values
    for degree in range(1, 5):
        image = apply_fn(taylor_term)
        factor = interval / degree
        taylor_term = jnp.stack([factor * image[1], -factor * image[0]])
        summed = summed + taylor_term
    return summed


def taylor_pair(values, apply_fn, first_len, second_len):
    first_sum = values
    second_sum = values
    taylor_term = values
    for degree in range(1, 5):
        image = apply_fn(taylor_term)
        factor = 1.0 / degree
        taylor_term = jnp.stack([factor * image[1], -factor * image[0]])
        first_sum = first_sum + first_len**degree * taylor_term
        second_sum = second_sum + second_len**degree * taylor_term
    return (first_sum, second_sum)


def density_potential(values, external):
    local_density = jnp.sum(values * values, axis=(0, 1))
    summed = lax.psum(local_density, "band")
    return external - exchange_coef * jnp.cbrt(summed)


def apply_each(values, potential):
    padded = with_halo(values, (("gx", 2), ("gy", 3)), 2)
    padded = jnp.pad(padded, ((0, 0), (0, 0), (0, 0), (0, 0), (2, 2)))
    return -0.5 * laplacian(padded) + potential * values


def body(orbitals, external):
    potential_now = density_potential(orbitals, external)

    def apply_now(values):
        return apply_each(values, potential_now)

    predicted, halfway = taylor_pair(orbitals, apply_now, step_length, step_length / 2)
    potential_next = density_potential(predicted, external)

    def apply_next(values):
        return apply_each(values, potential_next)

    result = taylor(halfway, apply_next, step_length / 2)
    return (result, potential_next)


def solution(mesh):
    in_specs = (P(None, "band", "gx", "gy", None), P("gx", "gy", None))
    out_specs = (P(None, "band", "gx", "gy", None), P("gx", "gy", None))
    return jax.shard_map(body, mesh=mesh, in_specs=in_specs, out_specs=out_specs, check_vma=False)
```

profile of v0, /device:TPU:0, one launch (start us, length us, event | category | flops | bytes accessed | tf_op | source)
XLA Modules:
  0.0 179.2 jit_solution(5112191598601688526)
XLA Ops:
  3.2 4.9 %collective-permute-start.1 = (f32[2,4,2,12,128]{4,2,3,1,0:T(2,128)S(1)}, f32[2,4,2,12,128]{4,2,3,1,0:T(2,128)S(1)}, u32[]{:S(2)}, u32[]{:S(2)}) collective-permute-start(f32[2,4,2,12,128]{4,2,3,1,0:T(2,128)S(1)} %get-tuple-element.65), channel_id=1, source_target_pairs={{0,16},{1,17},{2,18},{3,19},{4,20},{5,21},{6,22},{7,23},{8,24},{9,... | collective-permute-start | bytes 294920 | tf_op jit(solution)/shard_map/ppermute | solution.py:21
  9.1 12.0 %psum.14 = f32[8,12,128]{2,0,1:T(8,128)S(1)} all-reduce(f32[8,12,128]{2,0,1:T(8,128)S(1)} %get-tuple-element.62), channel_id=1, replica_groups=mesh['gx'=2,'gy'=4,'band'=4] {'band'}, use_global_device_ids=true, to_apply=%region_1.0 | all-reduce | flops 12288 | bytes 98304 | tf_op jit(solution)/shard_map/psum | solution.py:83
  22.9 3.5 %collective-permute-start.3 = (f32[2,4,12,2,128]{4,2,3,1,0:T(8,128)S(1)}, f32[2,4,12,2,128]{4,2,3,1,0:T(8,128)S(1)}, u32[]{:S(2)}, u32[]{:S(2)}) collective-permute-start(f32[2,4,12,2,128]{4,2,3,1,0:T(8,128)S(1)} %get-tuple-element.18), channel_id=1, source_target_pairs={{0,4},{4,8},{8,12},{1,5},{5,9},{9,13},{2,6},{6,10},{10,14},{3,7},{... | collective-permute-start | bytes 294920 | tf_op jit(solution)/shard_map/ppermute | solution.py:21
  29.0 4.3 %collective-permute-done.2 = f32[2,4,12,2,128]{4,2,3,1,0:T(8,128)S(1)} collective-permute-done((f32[2,4,12,2,128]{4,2,3,1,0:T(8,128)S(1)}, f32[2,4,12,2,128]{4,2,3,1,0:T(8,128)S(1)}, u32[]{:S(2)}, u32[]{:S(2)}) %collective-permute-start.2) | collective-permute-done | bytes 98336 | tf_op jit(solution)/shard_map/ppermute | solution.py:23
  39.1 4.3 %collective-permute-done.4 = f32[2,4,2,12,128]{4,2,3,1,0:T(2,128)S(1)} collective-permute-done((f32[2,4,2,12,128]{4,2,3,1,0:T(2,128)S(1)}, f32[2,4,2,12,128]{4,2,3,1,0:T(2,128)S(1)}, u32[]{:S(2)}, u32[]{:S(2)}) %collective-permute-start.4) | collective-permute-done | bytes 98336 | tf_op jit(solution)/shard_map/ppermute | solution.py:23
  43.5 3.5 %collective-permute-start.7 = (f32[2,4,12,2,128]{4,2,3,1,0:T(8,128)S(1)}, f32[2,4,12,2,128]{4,2,3,1,0:T(8,128)S(1)}, u32[]{:S(2)}, u32[]{:S(2)}) collective-permute-start(f32[2,4,12,2,128]{4,2,3,1,0:T(8,128)S(1)} %get-tuple-element.16), channel_id=1, source_target_pairs={{0,4},{4,8},{8,12},{1,5},{5,9},{9,13},{2,6},{6,10},{10,14},{3,7},{... | collective-permute-start | bytes 294920 | tf_op jit(solution)/shard_map/ppermute | solution.py:21
  49.5 4.4 %collective-permute-done.6 = f32[2,4,12,2,128]{4,2,3,1,0:T(8,128)S(1)} collective-permute-done((f32[2,4,12,2,128]{4,2,3,1,0:T(8,128)S(1)}, f32[2,4,12,2,128]{4,2,3,1,0:T(8,128)S(1)}, u32[]{:S(2)}, u32[]{:S(2)}) %collective-permute-start.6) | collective-permute-done | bytes 98336 | tf_op jit(solution)/shard_map/ppermute | solution.py:23
  59.4 4.3 %collective-permute-done.8 = f32[2,4,2,12,128]{4,2,3,1,0:T(2,128)S(1)} collective-permute-done((f32[2,4,2,12,128]{4,2,3,1,0:T(2,128)S(1)}, f32[2,4,2,12,128]{4,2,3,1,0:T(2,128)S(1)}, u32[]{:S(2)}, u32[]{:S(2)}) %collective-permute-start.8) | collective-permute-done | bytes 98336 | tf_op jit(solution)/shard_map/ppermute | solution.py:23
  63.8 3.5 %collective-permute-start.11 = (f32[2,4,12,2,128]{4,2,3,1,0:T(8,128)S(1)}, f32[2,4,12,2,128]{4,2,3,1,0:T(8,128)S(1)}, u32[]{:S(2)}, u32[]{:S(2)}) collective-permute-start(f32[2,4,12,2,128]{4,2,3,1,0:T(8,128)S(1)} %get-tuple-element.14), channel_id=1, source_target_pairs={{0,4},{4,8},{8,12},{1,5},{5,9},{9,13},{2,6},{6,10},{10,14},{3,7},{... | collective-permute-start | bytes 294920 | tf_op jit(solution)/shard_map/ppermute | solution.py:21
  69.8 4.4 %collective-permute-done.10 = f32[2,4,12,2,128]{4,2,3,1,0:T(8,128)S(1)} collective-permute-done((f32[2,4,12,2,128]{4,2,3,1,0:T(8,128)S(1)}, f32[2,4,12,2,128]{4,2,3,1,0:T(8,128)S(1)}, u32[]{:S(2)}, u32[]{:S(2)}) %collective-permute-start.10) | collective-permute-done | bytes 98336 | tf_op jit(solution)/shard_map/ppermute | solution.py:23
  79.7 4.3 %collective-permute-done.12 = f32[2,4,2,12,128]{4,2,3,1,0:T(2,128)S(1)} collective-permute-done((f32[2,4,2,12,128]{4,2,3,1,0:T(2,128)S(1)}, f32[2,4,2,12,128]{4,2,3,1,0:T(2,128)S(1)}, u32[]{:S(2)}, u32[]{:S(2)}) %collective-permute-start.12) | collective-permute-done | bytes 98336 | tf_op jit(solution)/shard_map/ppermute | solution.py:23
  84.0 1.9 %collective-permute-start.15 = (f32[2,4,12,2,128]{4,2,3,1,0:T(8,128)S(1)}, f32[2,4,12,2,128]{4,2,3,1,0:T(8,128)S(1)}, u32[]{:S(2)}, u32[]{:S(2)}) collective-permute-start(f32[2,4,12,2,128]{4,2,3,1,0:T(8,128)S(1)} %get-tuple-element.12), channel_id=1, source_target_pairs={{0,4},{4,8},{8,12},{1,5},{5,9},{9,13},{2,6},{6,10},{10,14},{3,7},{... | collective-permute-start | bytes 294920 | tf_op jit(solution)/shard_map/ppermute | solution.py:21
  88.5 4.4 %collective-permute-done.14 = f32[2,4,12,2,128]{4,2,3,1,0:T(8,128)S(1)} collective-permute-done((f32[2,4,12,2,128]{4,2,3,1,0:T(8,128)S(1)}, f32[2,4,12,2,128]{4,2,3,1,0:T(8,128)S(1)}, u32[]{:S(2)}, u32[]{:S(2)}) %collective-permute-start.14) | collective-permute-done | bytes 98336 | tf_op jit(solution)/shard_map/ppermute | solution.py:23
  96.2 4.6 %collective-permute-start.17 = (f32[2,4,2,12,128]{4,2,3,1,0:T(2,128)S(1)}, f32[2,4,2,12,128]{4,2,3,1,0:T(2,128)S(1)}, u32[]{:S(2)}, u32[]{:S(2)}) collective-permute-start(f32[2,4,2,12,128]{4,2,3,1,0:T(2,128)S(1)} %get-tuple-element.41), channel_id=1, source_target_pairs={{0,16},{1,17},{2,18},{3,19},{4,20},{5,21},{6,22},{7,23},{8,24},{9,... | collective-permute-start | bytes 294920 | tf_op jit(solution)/shard_map/ppermute | solution.py:21
  100.8 10.5 %psum.15 = f32[8,12,128]{2,0,1:T(8,128)S(1)} all-reduce(f32[8,12,128]{2,0,1:T(8,128)S(1)} %get-tuple-element.2), channel_id=1, replica_groups=mesh['gx'=2,'gy'=4,'band'=4] {'band'}, use_global_device_ids=true, to_apply=%region_3.4 | all-reduce | flops 12288 | bytes 98304 | tf_op jit(solution)/shard_map/psum | solution.py:83
  115.9 4.3 %collective-permute-done.18 = f32[2,4,12,2,128]{4,2,3,1,0:T(8,128)S(1)} collective-permute-done((f32[2,4,12,2,128]{4,2,3,1,0:T(8,128)S(1)}, f32[2,4,12,2,128]{4,2,3,1,0:T(8,128)S(1)}, u32[]{:S(2)}, u32[]{:S(2)}) %collective-permute-start.18) | collective-permute-done | bytes 98336 | tf_op jit(solution)/shard_map/ppermute | solution.py:23
  126.0 4.3 %collective-permute-done.20 = f32[2,4,2,12,128]{4,2,3,1,0:T(2,128)S(1)} collective-permute-done((f32[2,4,2,12,128]{4,2,3,1,0:T(2,128)S(1)}, f32[2,4,2,12,128]{4,2,3,1,0:T(2,128)S(1)}, u32[]{:S(2)}, u32[]{:S(2)}) %collective-permute-start.20) | collective-permute-done | bytes 98336 | tf_op jit(solution)/shard_map/ppermute | solution.py:23
  134.8 4.4 %collective-permute-done.22 = f32[2,4,12,2,128]{4,2,3,1,0:T(8,128)S(1)} collective-permute-done((f32[2,4,12,2,128]{4,2,3,1,0:T(8,128)S(1)}, f32[2,4,12,2,128]{4,2,3,1,0:T(8,128)S(1)}, u32[]{:S(2)}, u32[]{:S(2)}) %collective-permute-start.22) | collective-permute-done | bytes 98336 | tf_op jit(solution)/shard_map/ppermute | solution.py:23
  144.7 4.3 %collective-permute-done.24 = f32[2,4,2,12,128]{4,2,3,1,0:T(2,128)S(1)} collective-permute-done((f32[2,4,2,12,128]{4,2,3,1,0:T(2,128)S(1)}, f32[2,4,2,12,128]{4,2,3,1,0:T(2,128)S(1)}, u32[]{:S(2)}, u32[]{:S(2)}) %collective-permute-start.24) | collective-permute-done | bytes 98336 | tf_op jit(solution)/shard_map/ppermute | solution.py:23
  149.0 1.9 %collective-permute-start.27 = (f32[2,4,12,2,128]{4,2,3,1,0:T(8,128)S(1)}, f32[2,4,12,2,128]{4,2,3,1,0:T(8,128)S(1)}, u32[]{:S(2)}, u32[]{:S(2)}) collective-permute-start(f32[2,4,12,2,128]{4,2,3,1,0:T(8,128)S(1)} %get-tuple-element.6), channel_id=1, source_target_pairs={{0,4},{4,8},{8,12},{1,5},{5,9},{9,13},{2,6},{6,10},{10,14},{3,7},{... | collective-permute-start | bytes 294920 | tf_op jit(solution)/shard_map/ppermute | solution.py:21
  153.5 4.4 %collective-permute-done.26 = f32[2,4,12,2,128]{4,2,3,1,0:T(8,128)S(1)} collective-permute-done((f32[2,4,12,2,128]{4,2,3,1,0:T(8,128)S(1)}, f32[2,4,12,2,128]{4,2,3,1,0:T(8,128)S(1)}, u32[]{:S(2)}, u32[]{:S(2)}) %collective-permute-start.26) | collective-permute-done | bytes 98336 | tf_op jit(solution)/shard_map/ppermute | solution.py:23
  163.4 4.3 %collective-permute-done.28 = f32[2,4,2,12,128]{4,2,3,1,0:T(2,128)S(1)} collective-permute-done((f32[2,4,2,12,128]{4,2,3,1,0:T(2,128)S(1)}, f32[2,4,2,12,128]{4,2,3,1,0:T(2,128)S(1)}, u32[]{:S(2)}, u32[]{:S(2)}) %collective-permute-start.28) | collective-permute-done | bytes 98336 | tf_op jit(solution)/shard_map/ppermute | solution.py:23
  167.7 1.9 %collective-permute-start.31 = (f32[2,4,12,2,128]{4,2,3,1,0:T(8,128)S(1)}, f32[2,4,12,2,128]{4,2,3,1,0:T(8,128)S(1)}, u32[]{:S(2)}, u32[]{:S(2)}) collective-permute-start(f32[2,4,12,2,128]{4,2,3,1,0:T(8,128)S(1)} %get-tuple-element.4), channel_id=1, source_target_pairs={{0,4},{4,8},{8,12},{1,5},{5,9},{9,13},{2,6},{6,10},{10,14},{3,7},{... | collective-permute-start | bytes 294920 | tf_op jit(solution)/shard_map/ppermute | solution.py:21
  172.2 4.4 %collective-permute-done.30 = f32[2,4,12,2,128]{4,2,3,1,0:T(8,128)S(1)} collective-permute-done((f32[2,4,12,2,128]{4,2,3,1,0:T(8,128)S(1)}, f32[2,4,12,2,128]{4,2,3,1,0:T(8,128)S(1)}, u32[]{:S(2)}, u32[]{:S(2)}) %collective-permute-start.30) | collective-permute-done | bytes 98336 | tf_op jit(solution)/shard_map/ppermute | solution.py:23
  (100 shorter events, 69.0 us)
Async XLA Ops:
  1.9 20.1 %collective-permute-start = (f32[2,4,2,12,128]{4,2,3,1,0:T(2,128)S(1)}, f32[2,4,2,12,128]{4,2,3,1,0:T(2,128)S(1)}, u32[]{:S(2)}, u32[]{:S(2)}) collective-permute-start(f32[2,4,2,12,128]{4,2,3,1,0:T(2,128)S(1)} %get-tuple-element.64), channel_id=1, source_target_pairs={{16,0},{17,1},{18,2},{19,3},{20,4},{21,5},{22,6},{23,7},{24,8},{25... | collective-permute-start | bytes 294920 | tf_op jit(solution)/shard_map/ppermute | solution.py:23
  3.2 18.8 %collective-permute-start.1 = (f32[2,4,2,12,128]{4,2,3,1,0:T(2,128)S(1)}, f32[2,4,2,12,128]{4,2,3,1,0:T(2,128)S(1)}, u32[]{:S(2)}, u32[]{:S(2)}) collective-permute-start(f32[2,4,2,12,128]{4,2,3,1,0:T(2,128)S(1)} %get-tuple-element.65), channel_id=1, source_target_pairs={{0,16},{1,17},{2,18},{3,19},{4,20},{5,21},{6,22},{7,23},{8,24},{9,... | collective-permute-start | bytes 294920 | tf_op jit(solution)/shard_map/ppermute | solution.py:21
  22.9 6.1 %collective-permute-start.3 = (f32[2,4,12,2,128]{4,2,3,1,0:T(8,128)S(1)}, f32[2,4,12,2,128]{4,2,3,1,0:T(8,128)S(1)}, u32[]{:S(2)}, u32[]{:S(2)}) collective-permute-start(f32[2,4,12,2,128]{4,2,3,1,0:T(8,128)S(1)} %get-tuple-element.18), channel_id=1, source_target_pairs={{0,4},{4,8},{8,12},{1,5},{5,9},{9,13},{2,6},{6,10},{10,14},{3,7},{... | collective-permute-start | bytes 294920 | tf_op jit(solution)/shard_map/ppermute | solution.py:21
  26.4 6.9 %collective-permute-start.2 = (f32[2,4,12,2,128]{4,2,3,1,0:T(8,128)S(1)}, f32[2,4,12,2,128]{4,2,3,1,0:T(8,128)S(1)}, u32[]{:S(2)}, u32[]{:S(2)}) collective-permute-start(f32[2,4,12,2,128]{4,2,3,1,0:T(8,128)S(1)} %get-tuple-element.19), channel_id=1, source_target_pairs={{4,0},{8,4},{12,8},{5,1},{9,5},{13,9},{6,2},{10,6},{14,10},{7,3},{... | collective-permute-start | bytes 294920 | tf_op jit(solution)/shard_map/ppermute | solution.py:23
  36.9 6.5 %collective-permute-start.4 = (f32[2,4,2,12,128]{4,2,3,1,0:T(2,128)S(1)}, f32[2,4,2,12,128]{4,2,3,1,0:T(2,128)S(1)}, u32[]{:S(2)}, u32[]{:S(2)}) collective-permute-start(f32[2,4,2,12,128]{4,2,3,1,0:T(2,128)S(1)} %get-tuple-element.59), channel_id=1, source_target_pairs={{16,0},{17,1},{18,2},{19,3},{20,4},{21,5},{22,6},{23,7},{24,8},{25... | collective-permute-start | bytes 294920 | tf_op jit(solution)/shard_map/ppermute | solution.py:23
  43.5 6.0 %collective-permute-start.7 = (f32[2,4,12,2,128]{4,2,3,1,0:T(8,128)S(1)}, f32[2,4,12,2,128]{4,2,3,1,0:T(8,128)S(1)}, u32[]{:S(2)}, u32[]{:S(2)}) collective-permute-start(f32[2,4,12,2,128]{4,2,3,1,0:T(8,128)S(1)} %get-tuple-element.16), channel_id=1, source_target_pairs={{0,4},{4,8},{8,12},{1,5},{5,9},{9,13},{2,6},{6,10},{10,14},{3,7},{... | collective-permute-start | bytes 294920 | tf_op jit(solution)/shard_map/ppermute | solution.py:21
  47.0 6.9 %collective-permute-start.6 = (f32[2,4,12,2,128]{4,2,3,1,0:T(8,128)S(1)}, f32[2,4,12,2,128]{4,2,3,1,0:T(8,128)S(1)}, u32[]{:S(2)}, u32[]{:S(2)}) collective-permute-start(f32[2,4,12,2,128]{4,2,3,1,0:T(8,128)S(1)} %get-tuple-element.17), channel_id=1, source_target_pairs={{4,0},{8,4},{12,8},{5,1},{9,5},{13,9},{6,2},{10,6},{14,10},{7,3},{... | collective-permute-start | bytes 294920 | tf_op jit(solution)/shard_map/ppermute | solution.py:23
  57.2 6.5 %collective-permute-start.8 = (f32[2,4,2,12,128]{4,2,3,1,0:T(2,128)S(1)}, f32[2,4,2,12,128]{4,2,3,1,0:T(2,128)S(1)}, u32[]{:S(2)}, u32[]{:S(2)}) collective-permute-start(f32[2,4,2,12,128]{4,2,3,1,0:T(2,128)S(1)} %get-tuple-element.53), channel_id=1, source_target_pairs={{16,0},{17,1},{18,2},{19,3},{20,4},{21,5},{22,6},{23,7},{24,8},{25... | collective-permute-start | bytes 294920 | tf_op jit(solution)/shard_map/ppermute | solution.py:23
  63.8 6.0 %collective-permute-start.11 = (f32[2,4,12,2,128]{4,2,3,1,0:T(8,128)S(1)}, f32[2,4,12,2,128]{4,2,3,1,0:T(8,128)S(1)}, u32[]{:S(2)}, u32[]{:S(2)}) collective-permute-start(f32[2,4,12,2,128]{4,2,3,1,0:T(8,128)S(1)} %get-tuple-element.14), channel_id=1, source_target_pairs={{0,4},{4,8},{8,12},{1,5},{5,9},{9,13},{2,6},{6,10},{10,14},{3,7},{... | collective-permute-start | bytes 294920 | tf_op jit(solution)/shard_map/ppermute | solution.py:21
  67.3 6.9 %collective-permute-start.10 = (f32[2,4,12,2,128]{4,2,3,1,0:T(8,128)S(1)}, f32[2,4,12,2,128]{4,2,3,1,0:T(8,128)S(1)}, u32[]{:S(2)}, u32[]{:S(2)}) collective-permute-start(f32[2,4,12,2,128]{4,2,3,1,0:T(8,128)S(1)} %get-tuple-element.15), channel_id=1, source_target_pairs={{4,0},{8,4},{12,8},{5,1},{9,5},{13,9},{6,2},{10,6},{14,10},{7,3},{... | collective-permute-start | bytes 294920 | tf_op jit(solution)/shard_map/ppermute | solution.py:23
  77.5 6.5 %collective-permute-start.12 = (f32[2,4,2,12,128]{4,2,3,1,0:T(2,128)S(1)}, f32[2,4,2,12,128]{4,2,3,1,0:T(2,128)S(1)}, u32[]{:S(2)}, u32[]{:S(2)}) collective-permute-start(f32[2,4,2,12,128]{4,2,3,1,0:T(2,128)S(1)} %get-tuple-element.47), channel_id=1, source_target_pairs={{16,0},{17,1},{18,2},{19,3},{20,4},{21,5},{22,6},{23,7},{24,8},{25... | collective-permute-start | bytes 294920 | tf_op jit(solution)/shard_map/ppermute | solution.py:23
  86.0 6.9 %collective-permute-start.14 = (f32[2,4,12,2,128]{4,2,3,1,0:T(8,128)S(1)}, f32[2,4,12,2,128]{4,2,3,1,0:T(8,128)S(1)}, u32[]{:S(2)}, u32[]{:S(2)}) collective-permute-start(f32[2,4,12,2,128]{4,2,3,1,0:T(8,128)S(1)} %get-tuple-element.13), channel_id=1, source_target_pairs={{4,0},{8,4},{12,8},{5,1},{9,5},{13,9},{6,2},{10,6},{14,10},{7,3},{... | collective-permute-start | bytes 294920 | tf_op jit(solution)/shard_map/ppermute | solution.py:23
  94.9 16.4 %collective-permute-start.16 = (f32[2,4,2,12,128]{4,2,3,1,0:T(2,128)S(1)}, f32[2,4,2,12,128]{4,2,3,1,0:T(2,128)S(1)}, u32[]{:S(2)}, u32[]{:S(2)}) collective-permute-start(f32[2,4,2,12,128]{4,2,3,1,0:T(2,128)S(1)} %get-tuple-element.40), channel_id=1, source_target_pairs={{16,0},{17,1},{18,2},{19,3},{20,4},{21,5},{22,6},{23,7},{24,8},{25... | collective-permute-start | bytes 294920 | tf_op jit(solution)/shard_map/ppermute | solution.py:23
  96.2 15.1 %collective-permute-start.17 = (f32[2,4,2,12,128]{4,2,3,1,0:T(2,128)S(1)}, f32[2,4,2,12,128]{4,2,3,1,0:T(2,128)S(1)}, u32[]{:S(2)}, u32[]{:S(2)}) collective-permute-start(f32[2,4,2,12,128]{4,2,3,1,0:T(2,128)S(1)} %get-tuple-element.41), channel_id=1, source_target_pairs={{0,16},{1,17},{2,18},{3,19},{4,20},{5,21},{6,22},{7,23},{8,24},{9,... | collective-permute-start | bytes 294920 | tf_op jit(solution)/shard_map/ppermute | solution.py:21
  111.4 4.5 %collective-permute-start.19 = (f32[2,4,12,2,128]{4,2,3,1,0:T(8,128)S(1)}, f32[2,4,12,2,128]{4,2,3,1,0:T(8,128)S(1)}, u32[]{:S(2)}, u32[]{:S(2)}) collective-permute-start(f32[2,4,12,2,128]{4,2,3,1,0:T(8,128)S(1)} %get-tuple-element.10), channel_id=1, source_target_pairs={{0,4},{4,8},{8,12},{1,5},{5,9},{9,13},{2,6},{6,10},{10,14},{3,7},{... | collective-permute-start | bytes 294920 | tf_op jit(solution)/shard_map/ppermute | solution.py:21
  113.3 6.9 %collective-permute-start.18 = (f32[2,4,12,2,128]{4,2,3,1,0:T(8,128)S(1)}, f32[2,4,12,2,128]{4,2,3,1,0:T(8,128)S(1)}, u32[]{:S(2)}, u32[]{:S(2)}) collective-permute-start(f32[2,4,12,2,128]{4,2,3,1,0:T(8,128)S(1)} %get-tuple-element.11), channel_id=1, source_target_pairs={{4,0},{8,4},{12,8},{5,1},{9,5},{13,9},{6,2},{10,6},{14,10},{7,3},{... | collective-permute-start | bytes 294920 | tf_op jit(solution)/shard_map/ppermute | solution.py:23
  123.8 6.5 %collective-permute-start.20 = (f32[2,4,2,12,128]{4,2,3,1,0:T(2,128)S(1)}, f32[2,4,2,12,128]{4,2,3,1,0:T(2,128)S(1)}, u32[]{:S(2)}, u32[]{:S(2)}) collective-permute-start(f32[2,4,2,12,128]{4,2,3,1,0:T(2,128)S(1)} %get-tuple-element.37), channel_id=1, source_target_pairs={{16,0},{17,1},{18,2},{19,3},{20,4},{21,5},{22,6},{23,7},{24,8},{25... | collective-permute-start | bytes 294920 | tf_op jit(solution)/shard_map/ppermute | solution.py:23
  130.3 4.4 %collective-permute-start.23 = (f32[2,4,12,2,128]{4,2,3,1,0:T(8,128)S(1)}, f32[2,4,12,2,128]{4,2,3,1,0:T(8,128)S(1)}, u32[]{:S(2)}, u32[]{:S(2)}) collective-permute-start(f32[2,4,12,2,128]{4,2,3,1,0:T(8,128)S(1)} %get-tuple-element.8), channel_id=1, source_target_pairs={{0,4},{4,8},{8,12},{1,5},{5,9},{9,13},{2,6},{6,10},{10,14},{3,7},{... | collective-permute-start | bytes 294920 | tf_op jit(solution)/shard_map/ppermute | solution.py:21
  132.3 6.9 %collective-permute-start.22 = (f32[2,4,12,2,128]{4,2,3,1,0:T(8,128)S(1)}, f32[2,4,12,2,128]{4,2,3,1,0:T(8,128)S(1)}, u32[]{:S(2)}, u32[]{:S(2)}) collective-permute-start(f32[2,4,12,2,128]{4,2,3,1,0:T(8,128)S(1)} %get-tuple-element.9), channel_id=1, source_target_pairs={{4,0},{8,4},{12,8},{5,1},{9,5},{13,9},{6,2},{10,6},{14,10},{7,3},{... | collective-permute-start | bytes 294920 | tf_op jit(solution)/shard_map/ppermute | solution.py:23
  142.5 6.5 %collective-permute-start.24 = (f32[2,4,2,12,128]{4,2,3,1,0:T(2,128)S(1)}, f32[2,4,2,12,128]{4,2,3,1,0:T(2,128)S(1)}, u32[]{:S(2)}, u32[]{:S(2)}) collective-permute-start(f32[2,4,2,12,128]{4,2,3,1,0:T(2,128)S(1)} %get-tuple-element.31), channel_id=1, source_target_pairs={{16,0},{17,1},{18,2},{19,3},{20,4},{21,5},{22,6},{23,7},{24,8},{25... | collective-permute-start | bytes 294920 | tf_op jit(solution)/shard_map/ppermute | solution.py:23
  149.0 4.4 %collective-permute-start.27 = (f32[2,4,12,2,128]{4,2,3,1,0:T(8,128)S(1)}, f32[2,4,12,2,128]{4,2,3,1,0:T(8,128)S(1)}, u32[]{:S(2)}, u32[]{:S(2)}) collective-permute-start(f32[2,4,12,2,128]{4,2,3,1,0:T(8,128)S(1)} %get-tuple-element.6), channel_id=1, source_target_pairs={{0,4},{4,8},{8,12},{1,5},{5,9},{9,13},{2,6},{6,10},{10,14},{3,7},{... | collective-permute-start | bytes 294920 | tf_op jit(solution)/shard_map/ppermute | solution.py:21
  151.0 6.9 %collective-permute-start.26 = (f32[2,4,12,2,128]{4,2,3,1,0:T(8,128)S(1)}, f32[2,4,12,2,128]{4,2,3,1,0:T(8,128)S(1)}, u32[]{:S(2)}, u32[]{:S(2)}) collective-permute-start(f32[2,4,12,2,128]{4,2,3,1,0:T(8,128)S(1)} %get-tuple-element.7), channel_id=1, source_target_pairs={{4,0},{8,4},{12,8},{5,1},{9,5},{13,9},{6,2},{10,6},{14,10},{7,3},{... | collective-permute-start | bytes 294920 | tf_op jit(solution)/shard_map/ppermute | solution.py:23
  161.2 6.5 %collective-permute-start.28 = (f32[2,4,2,12,128]{4,2,3,1,0:T(2,128)S(1)}, f32[2,4,2,12,128]{4,2,3,1,0:T(2,128)S(1)}, u32[]{:S(2)}, u32[]{:S(2)}) collective-permute-start(f32[2,4,2,12,128]{4,2,3,1,0:T(2,128)S(1)} %get-tuple-element.25), channel_id=1, source_target_pairs={{16,0},{17,1},{18,2},{19,3},{20,4},{21,5},{22,6},{23,7},{24,8},{25... | collective-permute-start | bytes 294920 | tf_op jit(solution)/shard_map/ppermute | solution.py:23
  169.7 6.9 %collective-permute-start.30 = (f32[2,4,12,2,128]{4,2,3,1,0:T(8,128)S(1)}, f32[2,4,12,2,128]{4,2,3,1,0:T(8,128)S(1)}, u32[]{:S(2)}, u32[]{:S(2)}) collective-permute-start(f32[2,4,12,2,128]{4,2,3,1,0:T(8,128)S(1)} %get-tuple-element.5), channel_id=1, source_target_pairs={{4,0},{8,4},{12,8},{5,1},{9,5},{13,9},{6,2},{10,6},{14,10},{7,3},{... | collective-permute-start | bytes 294920 | tf_op jit(solution)/shard_map/ppermute | solution.py:23
  (11 other events, 147.1 us)
where the time goes:
time: 180 us; the launch traced here: 179 us
  waiting for transfers between devices  74.4 us (41%)
  starting transfers between devices  59.8 us (33%)
  blocking collectives  22.5 us (12%)
  other arithmetic  19.8 us (11%)
    ppermute x16, waiting for transfers between devices, with_halo(): lax.ppermute(head, axis, [((i + 1) % count, i) for i in range(ends)])  60.7 us
    ppermute x16, starting transfers between devices, with_halo(): lax.ppermute(tail, axis, [(i, (i + 1) % count) for i in range(ends)])  38.9 us
    psum x2, blocking collectives, density_potential(): summed = lax.psum(local_density, 'band')  22.5 us
    ppermute x16, starting transfers between devices, with_halo(): lax.ppermute(head, axis, [((i + 1) % count, i) for i in range(ends)])  20.9 us
    ppermute x16, waiting for transfers between devices, with_halo(): lax.ppermute(tail, axis, [(i, (i + 1) % count) for i in range(ends)])  13.7 us
    concatenate x22, other arithmetic, with_halo(): jnp.concatenate([lax.ppermute(tail, axis, [(i, (i + 1) % count) for i in...  10.4 us
    add x8, other arithmetic, apply_each(): return -0.5 * laplacian(padded) + potential * values  5.72 us
  transfers between devices with their start and end apart: 32, of which 28 were waited for; matrix products, arithmetic and copies ran while one was open for 2% of the time, Pallas kernels for 0%

commit v1 on v0

v1 whole, which is shorter than its diff:
```python
import functools

import jax
import jax.numpy as jnp
from jax import lax
from jax.experimental import pallas as pl
from jax.experimental.pallas import tpu as pltpu
from jax.sharding import PartitionSpec as P

step_length = 0.15
exchange_coef = 0.7386
centre_weight = -2.5
near_weight = 4.0 / 3.0
far_weight = -1.0 / 12.0
MESH = pl.DeviceIdType.MESH


def cube_root(d):
    guess = jnp.exp(jnp.log(d) * (1.0 / 3.0))
    better = guess - (guess - d / (guess * guess)) * (1.0 / 3.0)
    return jnp.where(d > 1e-30, better, guess)


def kernel(counts, orb_ref, ext_ref, out_ref, pot_ref, terms, pot_wide, density, x_send, x_recv, y_send, y_recv, d_send, d_recv):
    n_x, n_y, n_b = counts
    nx, ny, nf, nz = orb_ref.shape
    gx = lax.axis_index("gx")
    gy = lax.axis_index("gy")
    gb = lax.axis_index("band")
    has = {
        ("gx", 0): gx > 0,
        ("gx", 1): gx < n_x - 1,
        ("gy", 0): gy > 0,
        ("gy", 1): gy < n_y - 1,
    }
    place = {"gx": gx, "gy": gy}
    sides = [("gx", 0), ("gx", 1), ("gy", 0), ("gy", 1)]
    peers = [lax.rem(gb + j, n_b) for j in range(1, n_b)]

    def target(side):
        axis, up = side
        return {axis: place[axis] + (1 if up else -1)}

    barrier = pltpu.get_barrier_semaphore()
    partners = n_b - 1
    for side in sides:
        partners = partners + has[side].astype(jnp.int32)

        @pl.when(has[side])
        def _():
            pl.semaphore_signal(barrier, inc=1, device_id=target(side), device_id_type=MESH)

    for peer in peers:
        pl.semaphore_signal(barrier, inc=1, device_id={"band": peer}, device_id_type=MESH)
    pl.semaphore_wait(barrier, partners)

    def halo_copy(step, side):
        axis, up = side
        if axis == "gx":
            near = pl.ds(nx if up else 2, 2)
            land = pl.ds(0 if up else nx + 2, 2)
            src_index = (near, pl.ds(2, ny))
            dst = terms.at[step, land, pl.ds(2, ny)]
            sems = (x_send, x_recv)
        else:
            near = pl.ds(ny if up else 2, 2)
            land = pl.ds(0 if up else ny + 2, 2)
            src_index = (pl.ds(2, nx), near)
            dst = terms.at[step, pl.ds(2, nx), land]
            sems = (y_send, y_recv)
        if step == 0:
            begin = (nx if axis == "gx" else ny) - 2 if up else 0
            if axis == "gx":
                src = orb_ref.at[pl.ds(begin, 2)]
            else:
                src = orb_ref.at[:, pl.ds(begin, 2)]
        else:
            src = terms.at[(step,) + src_index]
        return pltpu.make_async_remote_copy(
            src_ref=src,
            dst_ref=dst,
            send_sem=sems[0].at[step, up],
            recv_sem=sems[1].at[step, 1 - up],
            device_id=target(side),
            device_id_type=MESH,
        )

    def start(step, axis):
        for up in (0, 1):

            @pl.when(has[(axis, up)])
            def _():
                halo_copy(step, (axis, up)).start()

    def await_halo(step, axis):
        for up in (0, 1):

            @pl.when(has[(axis, up)])
            def _():
                sems = (x_send, x_recv) if axis == "gx" else (y_send, y_recv)
                land = (
                    terms.at[step, pl.ds(nx + 2 if up else 0, 2), pl.ds(2, ny)]
                    if axis == "gx"
                    else terms.at[step, pl.ds(2, nx), pl.ds(ny + 2 if up else 0, 2)]
                )
                pltpu.make_async_remote_copy(
                    src_ref=land,
                    dst_ref=land,
                    send_sem=sems[0].at[step, up],
                    recv_sem=sems[1].at[step, up],
                    device_id=target((axis, up)),
                    device_id_type=MESH,
                ).wait_recv()

    def density_copy(which, j):
        return pltpu.make_async_remote_copy(
            src_ref=density.at[which, 0],
            dst_ref=density.at[which, n_b - 1 - j],
            send_sem=d_send.at[which, j],
            recv_sem=d_recv.at[which, n_b - 2 - j],
            device_id={"band": peers[j]},
            device_id_type=MESH,
        )

    def start_density(which):
        for j in range(n_b - 1):
            density_copy(which, j).start()

    def finish_potential(which):
        for slot in range(1, n_b):
            pltpu.make_async_remote_copy(
                src_ref=density.at[which, slot],
                dst_ref=density.at[which, slot],
                send_sem=d_send.at[which, slot - 1],
                recv_sem=d_recv.at[which, slot - 1],
                device_id={"band": peers[slot - 1]},
                device_id_type=MESH,
            ).wait_recv()

        def row(x, carry):
            total = density[which, 0, x]
            for slot in range(1, n_b):
                total = total + density[which, slot, x]
            pot = ext_ref[x] - exchange_coef * cube_root(total)
            if which == 1:
                pot_ref[x] = pot
            wide = pot - 1.5 * centre_weight
            for y in range(ny):
                pot_wide[x, y] = jnp.broadcast_to(wide[y : y + 1], (nf, nz))
            return carry

        lax.fori_loop(0, nx, row, 0)

    start(0, "gx")
    start(0, "gy")

    def load_row(x, carry):
        block = orb_ref[x]
        terms[0, x + 2, pl.ds(2, ny)] = block
        density[0, 0, x] = jnp.sum(block * block, axis=1)
        return carry

    lax.fori_loop(0, nx, load_row, 0)
    start_density(0)

    for side in sides:
        axis, up = side

        @pl.when(jnp.logical_not(has[side]))
        def _():
            def clear(step, carry):
                if axis == "gx":
                    shape = (2, ny, nf, nz)
                    terms[step, pl.ds(nx + 2 if up else 0, 2), pl.ds(2, ny)] = jnp.zeros(shape, jnp.float32)
                else:
                    shape = (nx, 2, nf, nz)
                    terms[step, pl.ds(2, nx), pl.ds(ny + 2 if up else 0, 2)] = jnp.zeros(shape, jnp.float32)
                return carry

            lax.fori_loop(0, 8, clear, 0)

    lane = lax.broadcasted_iota(jnp.int32, (nf, nz), 1)
    near = -0.5 * near_weight
    far = -0.5 * far_weight
    below1 = jnp.where(lane >= 1, near, 0.0)
    above1 = jnp.where(lane < nz - 1, near, 0.0)
    below2 = jnp.where(lane >= 2, far, 0.0)
    above2 = jnp.where(lane < nz - 2, far, 0.0)
    half = nf // 2
    field = lax.broadcasted_iota(jnp.int32, (nf, nz), 0)
    turn_sign = jnp.where(field < half, 1.0, -1.0)

    def turned(v):
        return jnp.concatenate([v[half:], v[:half]], axis=0) * turn_sign

    def image(step, x, y):
        c = terms[step, x + 2, y + 2]
        one = (terms[step, x + 1, y + 2] + terms[step, x + 3, y + 2]) + (
            terms[step, x + 2, y + 1] + terms[step, x + 2, y + 3]
        )
        two = (terms[step, x, y + 2] + terms[step, x + 4, y + 2]) + (
            terms[step, x + 2, y] + terms[step, x + 2, y + 4]
        )
        total = pot_wide[x, y] * c + near * one + far * two
        total = total + pltpu.roll(c, 1, 1) * below1 + pltpu.roll(c, nz - 1, 1) * above1
        return total + (pltpu.roll(c, 2, 1) * below2 + pltpu.roll(c, nz - 2, 1) * above2)

    def combine(parts, s):
        even = parts[0] + (-(s**2) / 2) * parts[2] + (s**4 / 24) * parts[4]
        odd = s * parts[1] + (-(s**3) / 6) * parts[3]
        return even + turned(odd)

    def advance(step, x_from, x_count):
        def row(i, carry):
            x = x_from + i
            squares = []
            for y in range(ny):
                new = image(step, x, y)
                if step % 4 < 3:
                    terms[step + 1, x + 2, y + 2] = new
                else:
                    parts = [terms[step - 3 + k, x + 2, y + 2] for k in range(4)] + [new]
                    if step == 3:
                        terms[4, x + 2, y + 2] = combine(parts, step_length / 2)
                        predicted = combine(parts, step_length)
                        squares.append(jnp.sum(predicted * predicted, axis=0, keepdims=True))
                    else:
                        out_ref[x, y] = combine(parts, step_length / 2)
            if step == 3:
                density[1, 0, x] = jnp.concatenate(squares, axis=0)
            return carry

        lax.fori_loop(0, x_count, row, 0)

    for step in range(8):
        if step % 4 == 0:
            finish_potential(step // 4)
        await_halo(step, "gx")
        await_halo(step, "gy")
        advance(step, 0, 2)
        advance(step, nx - 2, 2)
        if step < 7:
            start(step + 1, "gx")
        advance(step, 2, nx - 4)
        if step < 7:
            start(step + 1, "gy")
        if step == 3:
            start_density(1)

    for step in range(8):
        for side in sides:

            @pl.when(has[side])
            def _():
                halo_copy(step, side).wait_send()

    for which in (0, 1):
        for j in range(n_b - 1):
            density_copy(which, j).wait_send()


def body(counts, orbitals, external):
    parts, bands, nx, ny, nz = orbitals.shape
    nf = parts * bands
    fields = jnp.transpose(orbitals.reshape(nf, nx, ny, nz), (1, 2, 0, 3))
    n_b = counts[2]
    dma = pltpu.SemaphoreType.DMA
    result, potential = pl.pallas_call(
        functools.partial(kernel, counts),
        out_shape=(
            jax.ShapeDtypeStruct((nx, ny, nf, nz), jnp.float32),
            jax.ShapeDtypeStruct((nx, ny, nz), jnp.float32),
        ),
        in_specs=[pl.BlockSpec(memory_space=pltpu.VMEM)] * 2,
        out_specs=(pl.BlockSpec(memory_space=pltpu.VMEM),) * 2,
        scratch_shapes=[
            pltpu.VMEM((8, nx + 4, ny + 4, nf, nz), jnp.float32),
            pltpu.VMEM((nx, ny, nf, nz), jnp.float32),
            pltpu.VMEM((2, n_b, nx, ny, nz), jnp.float32),
            dma((8, 2)),
            dma((8, 2)),
            dma((8, 2)),
            dma((8, 2)),
            dma((2, n_b - 1)),
            dma((2, n_b - 1)),
        ],
        compiler_params=pltpu.CompilerParams(
            collective_id=0, has_side_effects=True, vmem_limit_bytes=40 * 1024 * 1024
        ),
    )(fields, external)
    result = jnp.transpose(result, (2, 0, 1, 3)).reshape(orbitals.shape)
    return (result, potential)


def solution(mesh):
    counts = (mesh.shape["gx"], mesh.shape["gy"], mesh.shape["band"])
    in_specs = (P(None, "band", "gx", "gy", None), P("gx", "gy", None))
    out_specs = (P(None, "band", "gx", "gy", None), P("gx", "gy", None))
    return jax.shard_map(
        functools.partial(body, counts), mesh=mesh, in_specs=in_specs, out_specs=out_specs, check_vma=False
    )
```

time: 180 us -> 46.5 us (0.26)
  waiting for transfers between devices: 74.4 us -> 0 us
  starting transfers between devices: 59.8 us -> 0 us
  Pallas kernels: 0 us -> 41.9 us
  blocking collectives: 22.5 us -> 0 us
  other arithmetic: 19.8 us -> 0 us
  local copies, waits for them, and re-layouts: 1.36 us -> 3.68 us
    ppermute x32 -> x0, waiting for transfers between devices: 74.4 us -> none  [the longest x16 60.7 us: with_halo(): lax.ppermute(head, axis, [((i + 1) % count, i) for i in range(ends)])]
    ppermute x32 -> x0, starting transfers between devices: 59.8 us -> none  [the longest x16 38.9 us: with_halo(): lax.ppermute(tail, axis, [(i, (i + 1) % count) for i in range(ends)])]
    pallas_call x0 -> x1, Pallas kernels: none -> 41.9 us  [body(): pl.pallas_call(functools.partial(kernel, counts), out_shape=(jax.ShapeDty...]
    psum x2 -> x0, blocking collectives: 22.5 us -> none  [density_potential(): summed = lax.psum(local_density, 'band')]
    concatenate x22 -> x0, other arithmetic: 10.4 us -> none  [with_halo(): jnp.concatenate([lax.ppermute(tail, axis, [(i, (i + 1) % count) for i in...]
    add x9 -> x0, other arithmetic: 6.59 us -> none  [the longest x8 5.72 us: apply_each(): return -0.5 * laplacian(padded) + potential * values]
    unnamed x6 -> x4, local copies, waits for them, and re-layouts: 0.02 us -> 3.68 us
  transfers between devices with their start and end apart: 32 -> 0, of which waited for: 28 -> 0; matrix products, arithmetic and copies ran while one was open for 2% -> 0% of each run, Pallas kernels for 0% -> 0%
where the time goes in v1:
time: 46.5 us; the launch traced here: 46.3 us
  Pallas kernels  41.9 us (90%)
  local copies, waits for them, and re-layouts  3.68 us (8%)
  between operations  0.64 us (1%)
    pallas_call x1, Pallas kernels, body(): pl.pallas_call(functools.partial(kernel, counts), out_shape=(jax.ShapeDty...  41.9 us
    unnamed x4, local copies, waits for them, and re-layouts  3.68 us

profile of v1, /device:TPU:0, one launch (start us, length us, event | category | flops | bytes accessed | tf_op | source)
XLA Modules:
  0.0 46.3 jit_solution(63757513356228646)
XLA Ops:
  0.6 0.8 %copy.5.ext_ref = f32[8,12,128]{2,1,0:T(8,128)S(1)} copy(f32[8,12,128]{2,0,1:T(8,128)} %param.3) | data formatting | bytes 98304 | tf_op args[1]
  1.4 1.3 %copy.4 = f32[2,4,8,12,128]{4,1,0,3,2:T(4,128)S(1)} copy(f32[2,4,8,12,128]{4,2,3,1,0:T(8,128)} %param.2) | data formatting | bytes 786432 | tf_op args[0]
  2.7 41.9 %shard_map.41 = (f32[8,12,8,128]{3,2,1,0:T(8,128)S(1)}, f32[8,12,128]{2,1,0:T(8,128)S(1)}) custom-call(f32[8,12,8,128]{3,2,1,0:T(8,128)S(1)} %bitcast.6, f32[8,12,128]{2,1,0:T(8,128)S(1)} %copy.5.ext_ref), custom_call_target="tpu_custom_call" | custom-call | tf_op jit(solution)/shard_map/pallas_call | solution.py:268
  44.6 1.0 %copy.6 = f32[2,4,8,12,128]{4,2,3,1,0:T(8,128)} copy(f32[2,4,8,12,128]{4,1,0,3,2:T(4,128)S(1)} %bitcast.7) | data formatting | bytes 786432
  45.6 0.6 %copy.7 = f32[8,12,128]{2,0,1:T(8,128)} copy(f32[8,12,128]{2,1,0:T(8,128)S(1)} %get-tuple-element.7) | data formatting | bytes 98304

commit v2 on v1

--- a/solution.py
+++ b/solution.py
@@ -54,90 +54,85 @@
         pl.semaphore_signal(barrier, inc=1, device_id={"band": peer}, device_id_type=MESH)
     pl.semaphore_wait(barrier, partners)
 
-    def halo_copy(step, side):
+    chunks = max(1, min(3, ny // 2))
+    x_cuts = [(j * (ny // chunks), ny // chunks + (ny % chunks if j == chunks - 1 else 0)) for j in range(chunks)]
+    y_cuts = [(0, 2), (nx - 2, 2), (2, nx - 4)]
+    order = sorted(range(chunks), key=lambda j: 0 if j in (0, chunks - 1) else 1)
+    sems = {"gx": (x_send, x_recv), "gy": (y_send, y_recv)}
+
+    def cells(axis, edge, piece):
+        if axis == "gx":
+            return pl.ds(edge, 2), pl.ds(2 + x_cuts[piece][0], x_cuts[piece][1])
+        return pl.ds(2 + y_cuts[piece][0], y_cuts[piece][1]), pl.ds(edge, 2)
+
+    def send_copy(step, side, piece):
         axis, up = side
-        if axis == "gx":
-            near = pl.ds(nx if up else 2, 2)
-            land = pl.ds(0 if up else nx + 2, 2)
-            src_index = (near, pl.ds(2, ny))
-            dst = terms.at[step, land, pl.ds(2, ny)]
-            sems = (x_send, x_recv)
+        extent = nx if axis == "gx" else ny
+        if step > 0:
+            src = terms.at[(step,) + cells(axis, extent if up else 2, piece)]
+        elif axis == "gx":
+            src = orb_ref.at[pl.ds(nx - 2 if up else 0, 2), pl.ds(*x_cuts[piece])]
         else:
-            near = pl.ds(ny if up else 2, 2)
-            land = pl.ds(0 if up else ny + 2, 2)
-            src_index = (pl.ds(2, nx), near)
-            dst = terms.at[step, pl.ds(2, nx), land]
-            sems = (y_send, y_recv)
-        if step == 0:
-            begin = (nx if axis == "gx" else ny) - 2 if up else 0
-            if axis == "gx":
-                src = orb_ref.at[pl.ds(begin, 2)]
-            else:
-                src = orb_ref.at[:, pl.ds(begin, 2)]
-        else:
-            src = terms.at[(step,) + src_index]
+            src = orb_ref.at[pl.ds(*y_cuts[piece]), pl.ds(ny - 2 if up else 0, 2)]
         return pltpu.make_async_remote_copy(
             src_ref=src,
-            dst_ref=dst,
-            send_sem=sems[0].at[step, up],
-            recv_sem=sems[1].at[step, 1 - up],
+            dst_ref=terms.at[(step,) + cells(axis, 0 if up else extent + 2, piece)],
+            send_sem=sems[axis][0].at[step, up, piece],
+            recv_sem=sems[axis][1].at[step, 1 - up, piece],
             device_id=target(side),
             device_id_type=MESH,
         )
 
-    def start(step, axis):
-        for up in (0, 1):
-
-            @pl.when(has[(axis, up)])
-            def _():
-                halo_copy(step, (axis, up)).start()
-
-    def await_halo(step, axis):
-        for up in (0, 1):
-
-            @pl.when(has[(axis, up)])
-            def _():
-                sems = (x_send, x_recv) if axis == "gx" else (y_send, y_recv)
-                land = (
-                    terms.at[step, pl.ds(nx + 2 if up else 0, 2), pl.ds(2, ny)]
-                    if axis == "gx"
-                    else terms.at[step, pl.ds(2, nx), pl.ds(ny + 2 if up else 0, 2)]
-                )
-                pltpu.make_async_remote_copy(
-                    src_ref=land,
-                    dst_ref=land,
-                    send_sem=sems[0].at[step, up],
-                    recv_sem=sems[1].at[step, up],
-                    device_id=target((axis, up)),
-                    device_id_type=MESH,
-                ).wait_recv()
-
-    def density_copy(which, j):
+    def start(step, side, piece):
+        @pl.when(has[side])
+        def _():
+            send_copy(step, side, piece).start()
+
+    def await_piece(step, side, piece):
+        axis, up = side
+        extent = nx if axis == "gx" else ny
+
+        @pl.when(has[side])
+        def _():
+            land = terms.at[(step,) + cells(axis, extent + 2 if up else 0, piece)]
+            pltpu.make_async_remote_copy(
+                src_ref=land,
+                dst_ref=land,
+                send_sem=sems[axis][0].at[step, up, piece],
+                recv_sem=sems[axis][1].at[step, up, piece],
+                device_id=target(side),
+                device_id_type=MESH,
+            ).wait_recv()
+
+    def density_copy(which, j, piece):
+        rows = pl.ds(*y_cuts[piece])
         return pltpu.make_async_remote_copy(
-            src_ref=density.at[which, 0],
-            dst_ref=density.at[which, n_b - 1 - j],
-            send_sem=d_send.at[which, j],
-            recv_sem=d_recv.at[which, n_b - 2 - j],
+            src_ref=density.at[which, 0, rows],
+            dst_ref=density.at[which, n_b - 1 - j, rows],
+            send_sem=d_send.at[which, j, piece],
+            recv_sem=d_recv.at[which, n_b - 2 - j, piece],
             device_id={"band": peers[j]},
             device_id_type=MESH,
         )
 
-    def start_density(which):
+    def start_density(which, piece):
         for j in range(n_b - 1):
-            density_copy(which, j).start()
-
-    def finish_potential(which):
+            density_copy(which, j, piece).start()
+
+    def finish_potential(which, piece):
+        rows = pl.ds(*y_cuts[piece])
         for slot in range(1, n_b):
             pltpu.make_async_remote_copy(
-                src_ref=density.at[which, slot],
-                dst_ref=density.at[which, slot],
-                send_sem=d_send.at[which, slot - 1],
-                recv_sem=d_recv.at[which, slot - 1],
+                src_ref=density.at[which, slot, rows],
+                dst_ref=density.at[which, slot, rows],
+                send_sem=d_send.at[which, slot - 1, piece],
+                recv_sem=d_recv.at[which, slot - 1, piece],
                 device_id={"band": peers[slot - 1]},
                 device_id_type=MESH,
             ).wait_recv()
 
-        def row(x, carry):
+        def row(i, carry):
+            x = y_cuts[piece][0] + i
             total = density[which, 0, x]
             for slot in range(1, n_b):
                 total = total + density[which, slot, x]
@@ -149,10 +144,14 @@
                 pot_wide[x, y] = jnp.broadcast_to(wide[y : y + 1], (nf, nz))
             return carry
 
-        lax.fori_loop(0, nx, row, 0)
-
-    start(0, "gx")
-    start(0, "gy")
+        lax.fori_loop(0, y_cuts[piece][1], row, 0)
+
+    for j in order:
+        for up in (0, 1):
+            start(0, ("gx", up), j)
+    for piece in range(3):
+        for up in (0, 1):
+            start(0, ("gy", up), piece)
 
     def load_row(x, carry):
         block = orb_ref[x]
@@ -160,8 +159,9 @@
         density[0, 0, x] = jnp.sum(block * block, axis=1)
         return carry
 
-    lax.fori_loop(0, nx, load_row, 0)
-    start_density(0)
+    for piece in range(3):
+        lax.fori_loop(y_cuts[piece][0], sum(y_cuts[piece]), load_row, 0)
+        start_density(0, piece)
 
     for side in sides:
         axis, up = side
@@ -210,15 +210,16 @@
         odd = s * parts[1] + (-(s**3) / 6) * parts[3]
         return even + turned(odd)
 
-    def advance(step, x_from, x_count):
+    def advance(step, x_from, x_count, runs):
         def row(i, carry):
             x = x_from + i
-            squares = []
-            for y in range(ny):
-                new = image(step, x, y)
-                if step % 4 < 3:
-                    terms[step + 1, x + 2, y + 2] = new
-                else:
+            for y_from, y_count in runs:
+                squares = []
+                for y in range(y_from, y_from + y_count):
+                    new = image(step, x, y)
+                    if step % 4 < 3:
+                        terms[step + 1, x + 2, y + 2] = new
+                        continue
                     parts = [terms[step - 3 + k, x + 2, y + 2] for k in range(4)] + [new]
                     if step == 3:
                         terms[4, x + 2, y + 2] = combine(parts, step_length / 2)
@@ -226,37 +227,58 @@
                         squares.append(jnp.sum(predicted * predicted, axis=0, keepdims=True))
                     else:
                         out_ref[x, y] = combine(parts, step_length / 2)
-            if step == 3:
-                density[1, 0, x] = jnp.concatenate(squares, axis=0)
+                if step == 3:
+                    density[1, 0, x, pl.ds(y_from, y_count)] = jnp.concatenate(squares, axis=0)
             return carry
 
         lax.fori_loop(0, x_count, row, 0)
 
     for step in range(8):
         if step % 4 == 0:
-            finish_potential(step // 4)
-        await_halo(step, "gx")
-        await_halo(step, "gy")
-        advance(step, 0, 2)
-        advance(step, nx - 2, 2)
+            finish_potential(step // 4, 0)
+            finish_potential(step // 4, 1)
+        for j in order:
+            edges = [("gy", up) for up, at in ((0, 0), (1, chunks - 1)) if at == j]
+            for up in (0, 1):
+                await_piece(step, ("gx", up), j)
+            for side in edges:
+                await_piece(step, side, 0)
+                await_piece(step, side, 1)
+            advance(step, 0, 2, [x_cuts[j]])
+            advance(step, nx - 2, 2, [x_cuts[j]])
+            if step < 7:
+                for up in (0, 1):
+                    start(step + 1, ("gx", up), j)
+                for side in edges:
+                    start(step + 1, side, 0)
+                    start(step + 1, side, 1)
+        if step == 3:
+            start_density(1, 0)
+            start_density(1, 1)
+        if step % 4 == 0:
+            finish_potential(step // 4, 2)
+        await_piece(step, ("gy", 0), 2)
+        await_piece(step, ("gy", 1), 2)
+        advance(step, 2, nx - 4, [(0, 2), (ny - 2, 2)])
         if step < 7:
-            start(step + 1, "gx")
-        advance(step, 2, nx - 4)
-        if step < 7:
-            start(step + 1, "gy")
+            start(step + 1, ("gy", 0), 2)
+            start(step + 1, ("gy", 1), 2)
+        advance(step, 2, nx - 4, [(2, ny - 4)])
         if step == 3:
-            start_density(1)
+            start_density(1, 2)
 
     for step in range(8):
         for side in sides:
 
             @pl.when(has[side])
             def _():
-                halo_copy(step, side).wait_send()
+                for piece in range(chunks if side[0] == "gx" else 3):
+                    send_copy(step, side, piece).wait_send()
 
     for which in (0, 1):
         for j in range(n_b - 1):
-            density_copy(which, j).wait_send()
+            for piece in range(3):
+                density_copy(which, j, piece).wait_send()
 
 
 def body(counts, orbitals, external):
@@ -277,12 +299,12 @@
             pltpu.VMEM((8, nx + 4, ny + 4, nf, nz), jnp.float32),
             pltpu.VMEM((nx, ny, nf, nz), jnp.float32),
             pltpu.VMEM((2, n_b, nx, ny, nz), jnp.float32),
-            dma((8, 2)),
-            dma((8, 2)),
-            dma((8, 2)),
-            dma((8, 2)),
-            dma((2, n_b - 1)),
-            dma((2, n_b - 1)),
+            dma((8, 2, 3)),
+            dma((8, 2, 3)),
+            dma((8, 2, 3)),
+            dma((8, 2, 3)),
+            dma((2, n_b - 1, 3)),
+            dma((2, n_b - 1, 3)),
         ],
         compiler_params=pltpu.CompilerParams(
             collective_id=0, has_side_effects=True, vmem_limit_bytes=40 * 1024 * 1024

time: 46.5 us -> 42.3 us (0.910)
  Pallas kernels: 41.9 us -> 37.8 us
    pallas_call x1, Pallas kernels: 41.9 us -> 37.8 us  [body(): pl.pallas_call(functools.partial(kernel, counts), out_shape=(jax.ShapeDty...]
where the time goes in v2:
time: 42.3 us; the launch traced here: 42.1 us
  Pallas kernels  37.8 us (89%)
  local copies, waits for them, and re-layouts  3.68 us (9%)
  between operations  0.64 us (2%)
    pallas_call x1, Pallas kernels, body(): pl.pallas_call(functools.partial(kernel, counts), out_shape=(jax.ShapeDty...  37.8 us
    unnamed x4, local copies, waits for them, and re-layouts  3.68 us

profile of v2, /device:TPU:0, one launch (start us, length us, event | category | flops | bytes accessed | tf_op | source)
XLA Modules:
  0.0 42.1 jit_solution(4298494942381507443)
XLA Ops:
  0.6 0.8 %copy.5.ext_ref = f32[8,12,128]{2,1,0:T(8,128)S(1)} copy(f32[8,12,128]{2,0,1:T(8,128)} %param.3) | data formatting | bytes 98304 | tf_op args[1]
  1.4 1.3 %copy.4 = f32[2,4,8,12,128]{4,1,0,3,2:T(4,128)S(1)} copy(f32[2,4,8,12,128]{4,2,3,1,0:T(8,128)} %param.2) | data formatting | bytes 786432 | tf_op args[0]
  2.7 37.8 %shard_map.41 = (f32[8,12,8,128]{3,2,1,0:T(8,128)S(1)}, f32[8,12,128]{2,1,0:T(8,128)S(1)}) custom-call(f32[8,12,8,128]{3,2,1,0:T(8,128)S(1)} %bitcast.6, f32[8,12,128]{2,1,0:T(8,128)S(1)} %copy.5.ext_ref), custom_call_target="tpu_custom_call" | custom-call | tf_op jit(solution)/shard_map/pallas_call | solution.py:290
  40.5 1.0 %copy.6 = f32[2,4,8,12,128]{4,2,3,1,0:T(8,128)} copy(f32[2,4,8,12,128]{4,1,0,3,2:T(4,128)S(1)} %bitcast.7) | data formatting | bytes 786432
  41.5 0.6 %copy.7 = f32[8,12,128]{2,0,1:T(8,128)} copy(f32[8,12,128]{2,1,0:T(8,128)S(1)} %get-tuple-element.7) | data formatting | bytes 98304

commit v3 on v2

v3 whole, which is shorter than its diff:
```python
import functools

import jax
import jax.numpy as jnp
from jax import lax
from jax.experimental import pallas as pl
from jax.experimental.pallas import tpu as pltpu
from jax.sharding import PartitionSpec as P

step_length = 0.15
exchange_coef = 0.7386
centre_weight = -2.5
near_weight = 4.0 / 3.0
far_weight = -1.0 / 12.0
MESH = pl.DeviceIdType.MESH


def cube_root(d):
    guess = jnp.exp(jnp.log(d) * (1.0 / 3.0))
    better = guess - (guess - d / (guess * guess)) * (1.0 / 3.0)
    return jnp.where(d > 1e-30, better, guess)


def kernel(counts, orb_hbm, ext_hbm, out_ref, pot_ref, *scratch):
    terms = scratch[:8]
    orb_ref, ext_ref, pot_wide, density, in_sem, x_send, x_recv, y_send, y_recv, d_send, d_recv = scratch[8:]
    n_x, n_y, n_b = counts
    nf, ny, nx, nz = orb_ref.shape
    gx = lax.axis_index("gx")
    gy = lax.axis_index("gy")
    gb = lax.axis_index("band")
    has = {
        ("gx", 0): gx > 0,
        ("gx", 1): gx < n_x - 1,
        ("gy", 0): gy > 0,
        ("gy", 1): gy < n_y - 1,
    }
    place = {"gx": gx, "gy": gy}
    sides = [("gx", 0), ("gx", 1), ("gy", 0), ("gy", 1)]
    peers = [lax.rem(gb + j, n_b) for j in range(1, n_b)]

    def target(side):
        axis, up = side
        return {axis: place[axis] + (1 if up else -1)}

    barrier = pltpu.get_barrier_semaphore()
    partners = n_b - 1
    for side in sides:
        partners = partners + has[side].astype(jnp.int32)

        @pl.when(has[side])
        def _():
            pl.semaphore_signal(barrier, inc=1, device_id=target(side), device_id_type=MESH)

    for peer in peers:
        pl.semaphore_signal(barrier, inc=1, device_id={"band": peer}, device_id_type=MESH)
    orb_in = pltpu.make_async_copy(orb_hbm, orb_ref, in_sem.at[0])
    orb_in.start()
    ext_in = pltpu.make_async_copy(ext_hbm, ext_ref, in_sem.at[1])
    ext_in.start()

    chunks = max(1, min(6, ny // 2))
    x_cuts = [(j * (ny // chunks), ny // chunks + (ny % chunks if j == chunks - 1 else 0)) for j in range(chunks)]
    y_cuts = [(0, 2), (nx - 2, 2), (2, nx - 4)]
    d_cuts = [(0, 2), (ny - 2, 2), (2, ny - 4)]
    order = sorted(range(chunks), key=lambda j: 0 if j in (0, chunks - 1) else 1)
    sems = {"gx": (x_send, x_recv), "gy": (y_send, y_recv)}

    def cells(axis, edge, piece):
        if axis == "gx":
            return pl.ds(edge, 2), pl.ds(2 + x_cuts[piece][0], x_cuts[piece][1])
        return pl.ds(2 + y_cuts[piece][0], y_cuts[piece][1]), pl.ds(edge, 2)

    def send_copy(step, side, piece):
        axis, up = side
        extent = nx if axis == "gx" else ny
        src = terms[step].at[cells(axis, extent if up else 2, piece)]
        return pltpu.make_async_remote_copy(
            src_ref=src,
            dst_ref=terms[step].at[cells(axis, 0 if up else extent + 2, piece)],
            send_sem=sems[axis][0].at[step, up, piece],
            recv_sem=sems[axis][1].at[step, 1 - up, piece],
            device_id=target(side),
            device_id_type=MESH,
        )

    def start(step, side, piece):
        @pl.when(has[side])
        def _():
            send_copy(step, side, piece).start()

    def await_piece(step, side, piece):
        axis, up = side
        extent = nx if axis == "gx" else ny

        @pl.when(has[side])
        def _():
            land = terms[step].at[cells(axis, extent + 2 if up else 0, piece)]
            pltpu.make_async_remote_copy(
                src_ref=land,
                dst_ref=land,
                send_sem=sems[axis][0].at[step, up, piece],
                recv_sem=sems[axis][1].at[step, up, piece],
                device_id=target(side),
                device_id_type=MESH,
            ).wait_recv()

    def density_copy(which, j, piece):
        rows = pl.ds(*d_cuts[piece])
        return pltpu.make_async_remote_copy(
            src_ref=density.at[which, 0, rows],
            dst_ref=density.at[which, n_b - 1 - j, rows],
            send_sem=d_send.at[which, j, piece],
            recv_sem=d_recv.at[which, n_b - 2 - j, piece],
            device_id={"band": peers[j]},
            device_id_type=MESH,
        )

    def start_density(which, piece):
        for j in range(n_b - 1):
            density_copy(which, j, piece).start()

    def finish_potential(which):
        for piece in range(3):
            rows = pl.ds(*d_cuts[piece])
            for slot in range(1, n_b):
                pltpu.make_async_remote_copy(
                    src_ref=density.at[which, slot, rows],
                    dst_ref=density.at[which, slot, rows],
                    send_sem=d_send.at[which, slot - 1, piece],
                    recv_sem=d_recv.at[which, slot - 1, piece],
                    device_id={"band": peers[slot - 1]},
                    device_id_type=MESH,
                ).wait_recv()
        total = density[which, 0]
        for slot in range(1, n_b):
            total = total + density[which, slot]
        pot = ext_ref[...] - exchange_coef * cube_root(total)
        if which == 1:
            pot_ref[...] = pot
        wide = pot - 1.5 * centre_weight
        for y in range(ny):
            for x in range(nx):
                pot_wide[x, y] = jnp.broadcast_to(wide[y, x : x + 1], (nf, nz))

    for side in sides:
        axis, up = side

        @pl.when(jnp.logical_not(has[side]))
        def _():
            for step in range(8):
                if axis == "gx":
                    shape = (2, ny, nf, nz)
                    terms[step][pl.ds(nx + 2 if up else 0, 2), pl.ds(2, ny)] = jnp.zeros(shape, jnp.float32)
                else:
                    shape = (nx, 2, nf, nz)
                    terms[step][pl.ds(2, nx), pl.ds(ny + 2 if up else 0, 2)] = jnp.zeros(shape, jnp.float32)

    orb_in.wait()
    for y in range(ny):
        block = orb_ref[:, y]
        terms[0][pl.ds(2, nx), y + 2] = jnp.swapaxes(block, 0, 1)
        density[0, 0, y] = jnp.sum(block * block, axis=0)
    pl.semaphore_wait(barrier, partners)
    for j in order:
        for up in (0, 1):
            start(0, ("gx", up), j)
    for piece in range(3):
        for up in (0, 1):
            start(0, ("gy", up), piece)
    for piece in range(3):
        start_density(0, piece)
    ext_in.wait()

    lane = lax.broadcasted_iota(jnp.int32, (nf, nz), 1)
    near = -0.5 * near_weight
    far = -0.5 * far_weight
    below1 = jnp.where(lane >= 1, near, 0.0)
    above1 = jnp.where(lane < nz - 1, near, 0.0)
    below2 = jnp.where(lane >= 2, far, 0.0)
    above2 = jnp.where(lane < nz - 2, far, 0.0)
    half = nf // 2
    field = lax.broadcasted_iota(jnp.int32, (nf, nz), 0)
    turn_sign = jnp.where(field < half, 1.0, -1.0)

    def turned(v):
        return jnp.concatenate([v[half:], v[:half]], axis=0) * turn_sign

    def image(step, x, y):
        t = terms[step]
        c = t[x + 2, y + 2]
        one = (t[x + 1, y + 2] + t[x + 3, y + 2]) + (
            t[x + 2, y + 1] + t[x + 2, y + 3]
        )
        two = (t[x, y + 2] + t[x + 4, y + 2]) + (
            t[x + 2, y] + t[x + 2, y + 4]
        )
        total = pot_wide[x, y] * c + near * one + far * two
        total = total + pltpu.roll(c, 1, 1) * below1 + pltpu.roll(c, nz - 1, 1) * above1
        return total + (pltpu.roll(c, 2, 1) * below2 + pltpu.roll(c, nz - 2, 1) * above2)

    def combine(parts, s):
        even = parts[0] + (-(s**2) / 2) * parts[2] + (s**4 / 24) * parts[4]
        odd = s * parts[1] + (-(s**3) / 6) * parts[3]
        return even + turned(odd)

    def advance(step, xs, ys):
        at = [(x, y) for x in xs for y in ys]
        new = [image(step, x, y) for x, y in at]
        if step % 4 < 3:
            for (x, y), value in zip(at, new):
                terms[step + 1][x + 2, y + 2] = value
            return
        parts = [[terms[step - 3 + k][x + 2, y + 2] for k in range(4)] + [value] for (x, y), value in zip(at, new)]
        halves = [combine(part, step_length / 2) for part in parts]
        if step == 7:
            for (x, y), value in zip(at, halves):
                out_ref[x, y] = value
            return
        predicted = [combine(part, step_length) for part in parts]
        squares = [jnp.sum(value * value, axis=0, keepdims=True) for value in predicted]
        for (x, y), value, square in zip(at, halves, squares):
            terms[4][x + 2, y + 2] = value
            density[1, 0, y, pl.ds(x, 1)] = square

    rim = [0, 1, nx - 2, nx - 1]
    for step in range(8):
        if step % 4 == 0:
            finish_potential(step // 4)
        for j in order:
            edges = [("gy", up) for up, at in ((0, 0), (1, chunks - 1)) if at == j]
            for up in (0, 1):
                await_piece(step, ("gx", up), j)
            for side in edges:
                await_piece(step, side, 0)
                await_piece(step, side, 1)
            advance(step, rim, range(x_cuts[j][0], sum(x_cuts[j])))
            if step < 7:
                for up in (0, 1):
                    start(step + 1, ("gx", up), j)
                for side in edges:
                    start(step + 1, side, 0)
                    start(step + 1, side, 1)
        await_piece(step, ("gy", 0), 2)
        await_piece(step, ("gy", 1), 2)
        advance(step, range(2, nx - 2), [0, 1, ny - 2, ny - 1])
        if step < 7:
            start(step + 1, ("gy", 0), 2)
            start(step + 1, ("gy", 1), 2)
        if step == 3:
            start_density(1, 0)
            start_density(1, 1)
        for x in range(2, nx - 2):
            advance(step, [x], range(2, ny - 2))
        if step == 3:
            start_density(1, 2)

    for step in range(8):
        for side in sides:

            @pl.when(has[side])
            def _():
                for piece in range(chunks if side[0] == "gx" else 3):
                    send_copy(step, side, piece).wait_send()

    for which in (0, 1):
        for j in range(n_b - 1):
            for piece in range(3):
                density_copy(which, j, piece).wait_send()


def body(counts, orbitals, external):
    parts, bands, nx, ny, nz = orbitals.shape
    nf = parts * bands
    fields = jnp.transpose(orbitals.reshape(nf, nx, ny, nz), (0, 2, 1, 3))
    n_b = counts[2]
    dma = pltpu.SemaphoreType.DMA
    result, potential = pl.pallas_call(
        functools.partial(kernel, counts),
        out_shape=(
            jax.ShapeDtypeStruct((nx, ny, nf, nz), jnp.float32),
            jax.ShapeDtypeStruct((ny, nx, nz), jnp.float32),
        ),
        in_specs=[pl.BlockSpec(memory_space=pl.ANY)] * 2,
        out_specs=(pl.BlockSpec(memory_space=pltpu.VMEM),) * 2,
        scratch_shapes=[
            *[pltpu.VMEM((nx + 4, ny + 4, nf, nz), jnp.float32)] * 8,
            pltpu.VMEM((nf, ny, nx, nz), jnp.float32),
            pltpu.VMEM((ny, nx, nz), jnp.float32),
            pltpu.VMEM((nx, ny, nf, nz), jnp.float32),
            pltpu.VMEM((2, n_b, ny, nx, nz), jnp.float32),
            dma((2,)),
            dma((8, 2, 6)),
            dma((8, 2, 6)),
            dma((8, 2, 3)),
            dma((8, 2, 3)),
            dma((2, n_b - 1, 3)),
            dma((2, n_b - 1, 3)),
        ],
        compiler_params=pltpu.CompilerParams(
            collective_id=0, has_side_effects=True, vmem_limit_bytes=40 * 1024 * 1024
        ),
    )(fields, jnp.swapaxes(external, 0, 1))
    result = jnp.transpose(result, (2, 0, 1, 3)).reshape(orbitals.shape)
    return (result, jnp.swapaxes(potential, 0, 1))


def solution(mesh):
    counts = (mesh.shape["gx"], mesh.shape["gy"], mesh.shape["band"])
    in_specs = (P(None, "band", "gx", "gy", None), P("gx", "gy", None))
    out_specs = (P(None, "band", "gx", "gy", None), P("gx", "gy", None))
    return jax.shard_map(
        functools.partial(body, counts), mesh=mesh, in_specs=in_specs, out_specs=out_specs, check_vma=False
    )
```

time: 42.3 us -> 41.4 us (0.979)
  Pallas kernels: 37.8 us -> 37.1 us
    pallas_call x1, Pallas kernels: 37.8 us -> 37.1 us  [body(): pl.pallas_call(functools.partial(kernel, counts), out_shape=(jax.ShapeDty...]
    unnamed x4 -> x6, local copies, waits for them, and re-layouts: 3.68 us -> 3.38 us
where the time goes in v3:
time: 41.4 us; the launch traced here: 41.2 us
  Pallas kernels  37.1 us (90%)
  local copies, waits for them, and re-layouts  3.38 us (8%)
  between operations  0.65 us (2%)
    pallas_call x1, Pallas kernels, body(): pl.pallas_call(functools.partial(kernel, counts), out_shape=(jax.ShapeDty...  37.1 us
    unnamed x6, local copies, waits for them, and re-layouts  3.38 us

profile of v3, /device:TPU:0, one launch (start us, length us, event | category | flops | bytes accessed | tf_op | source)
XLA Modules:
  0.0 41.2 jit_solution(501708412926873747)
XLA Ops:
  0.6 0.0 copy-start
  0.6 1.0 %copy-done = f32[2,4,8,12,128]{4,2,3,1,0:T(8,128)S(1)} copy-done((f32[2,4,8,12,128]{4,2,3,1,0:T(8,128)S(1)}, f32[2,4,8,12,128]{4,2,3,1,0:T(8,128)}, u32[]{:S(2)}) %copy-start) | copy-done | bytes 393240
  1.6 0.0 copy-start.1
  1.6 0.8 %copy-done.1 = f32[8,12,128]{2,0,1:T(8,128)S(1)} copy-done((f32[8,12,128]{2,0,1:T(8,128)S(1)}, f32[8,12,128]{2,0,1:T(8,128)}, u32[]{:S(2)}) %copy-start.1) | copy-done | bytes 49176
  2.4 37.1 %shard_map.41 = (f32[8,12,8,128]{3,2,1,0:T(8,128)S(1)}, f32[12,8,128]{2,1,0:T(8,128)S(1)}) custom-call(f32[8,12,8,128]{3,2,1,0:T(8,128)S(1)} %bitcast.8, f32[12,8,128]{2,1,0:T(8,128)S(1)} %bitcast.10), custom_call_target="tpu_custom_call" | custom-call | tf_op jit(solution)/shard_map/pallas_call | solution.py:278
  39.6 1.0 %copy.4 = f32[2,4,8,12,128]{4,2,3,1,0:T(8,128)} copy(f32[2,4,8,12,128]{4,1,0,3,2:T(4,128)S(1)} %bitcast.9) | data formatting | bytes 786432
  40.6 0.6 %copy.6 = f32[8,12,128]{2,0,1:T(8,128)} copy(f32[8,12,128]{2,0,1:T(8,128)S(1)} %bitcast.11) | data formatting | bytes 98304
Async XLA Ops:
  0.6 1.0 %copy-start = (f32[2,4,8,12,128]{4,2,3,1,0:T(8,128)S(1)}, f32[2,4,8,12,128]{4,2,3,1,0:T(8,128)}, u32[]{:S(2)}) copy-start(f32[2,4,8,12,128]{4,2,3,1,0:T(8,128)} %param.2) | copy-start | bytes 1179652
  1.6 0.8 %copy-start.1 = (f32[8,12,128]{2,0,1:T(8,128)S(1)}, f32[8,12,128]{2,0,1:T(8,128)}, u32[]{:S(2)}) copy-start(f32[8,12,128]{2,0,1:T(8,128)} %param.3) | copy-start | bytes 147460

commit v4 on v3

--- a/solution.py
+++ b/solution.py
@@ -36,12 +36,17 @@
         ("gy", 1): gy < n_y - 1,
     }
     place = {"gx": gx, "gy": gy}
-    sides = [("gx", 0), ("gx", 1), ("gy", 0), ("gy", 1)]
+    if n_x == 2:
+        x_sides = [("gx", 1 - gx)]
+    else:
+        x_sides = [("gx", 0), ("gx", 1)]
+    y_sides = [("gy", 0), ("gy", 1)]
+    sides = [("gx", 0), ("gx", 1)] + y_sides
     peers = [lax.rem(gb + j, n_b) for j in range(1, n_b)]
 
     def target(side):
         axis, up = side
-        return {axis: place[axis] + (1 if up else -1)}
+        return {axis: place[axis] + (2 * up - 1)}
 
     barrier = pltpu.get_barrier_semaphore()
     partners = n_b - 1
@@ -61,7 +66,8 @@
 
     chunks = max(1, min(6, ny // 2))
     x_cuts = [(j * (ny // chunks), ny // chunks + (ny % chunks if j == chunks - 1 else 0)) for j in range(chunks)]
-    y_cuts = [(0, 2), (nx - 2, 2), (2, nx - 4)]
+    mid = (nx - 4) // 2
+    y_cuts = [(0, 2), (nx - 2, 2), (2, mid), (2 + mid, nx - 4 - mid)]
     d_cuts = [(0, 2), (ny - 2, 2), (2, ny - 4)]
     order = sorted(range(chunks), key=lambda j: 0 if j in (0, chunks - 1) else 1)
     sems = {"gx": (x_send, x_recv), "gy": (y_send, y_recv)}
@@ -71,39 +77,55 @@
             return pl.ds(edge, 2), pl.ds(2 + x_cuts[piece][0], x_cuts[piece][1])
         return pl.ds(2 + y_cuts[piece][0], y_cuts[piece][1]), pl.ds(edge, 2)
 
+    def pick(up, high, low):
+        if isinstance(up, int):
+            return high if up else low
+        return low + up * (high - low)
+
     def send_copy(step, side, piece):
         axis, up = side
         extent = nx if axis == "gx" else ny
-        src = terms[step].at[cells(axis, extent if up else 2, piece)]
         return pltpu.make_async_remote_copy(
-            src_ref=src,
-            dst_ref=terms[step].at[cells(axis, 0 if up else extent + 2, piece)],
+            src_ref=terms[step].at[cells(axis, pick(up, extent, 2), piece)],
+            dst_ref=terms[step].at[cells(axis, pick(up, 0, extent + 2), piece)],
             send_sem=sems[axis][0].at[step, up, piece],
             recv_sem=sems[axis][1].at[step, 1 - up, piece],
             device_id=target(side),
             device_id_type=MESH,
         )
 
-    def start(step, side, piece):
-        @pl.when(has[side])
-        def _():
-            send_copy(step, side, piece).start()
-
-    def await_piece(step, side, piece):
+    def recv_copy(step, side, piece):
         axis, up = side
         extent = nx if axis == "gx" else ny
-
-        @pl.when(has[side])
-        def _():
-            land = terms[step].at[cells(axis, extent + 2 if up else 0, piece)]
-            pltpu.make_async_remote_copy(
-                src_ref=land,
-                dst_ref=land,
-                send_sem=sems[axis][0].at[step, up, piece],
-                recv_sem=sems[axis][1].at[step, up, piece],
-                device_id=target(side),
-                device_id_type=MESH,
-            ).wait_recv()
+        land = terms[step].at[cells(axis, pick(up, extent + 2, 0), piece)]
+        return pltpu.make_async_remote_copy(
+            src_ref=land,
+            dst_ref=land,
+            send_sem=sems[axis][0].at[step, up, piece],
+            recv_sem=sems[axis][1].at[step, up, piece],
+            device_id=target(side),
+            device_id_type=MESH,
+        )
+
+    def each(side, act):
+        if side[0] == "gx" and n_x == 2:
+            act()
+        else:
+            pl.when(has[side])(act)
+
+    def start(step, side, pieces):
+        def act():
+            for piece in pieces:
+                send_copy(step, side, piece).start()
+
+        each(side, act)
+
+    def await_pieces(step, side, pieces):
+        def act():
+            for piece in pieces:
+                recv_copy(step, side, piece).wait_recv()
+
+        each(side, act)
 
     def density_copy(which, j, piece):
         rows = pl.ds(*d_cuts[piece])
@@ -162,12 +184,10 @@
         terms[0][pl.ds(2, nx), y + 2] = jnp.swapaxes(block, 0, 1)
         density[0, 0, y] = jnp.sum(block * block, axis=0)
     pl.semaphore_wait(barrier, partners)
-    for j in order:
-        for up in (0, 1):
-            start(0, ("gx", up), j)
-    for piece in range(3):
-        for up in (0, 1):
-            start(0, ("gy", up), piece)
+    for side in x_sides:
+        start(0, side, order)
+    for side in y_sides:
+        start(0, side, range(4))
     for piece in range(3):
         start_density(0, piece)
     ext_in.wait()
@@ -227,41 +247,42 @@
     for step in range(8):
         if step % 4 == 0:
             finish_potential(step // 4)
-        for j in order:
+        for n, j in enumerate(order):
             edges = [("gy", up) for up, at in ((0, 0), (1, chunks - 1)) if at == j]
-            for up in (0, 1):
-                await_piece(step, ("gx", up), j)
+            for side in x_sides:
+                await_pieces(step, side, [j])
             for side in edges:
-                await_piece(step, side, 0)
-                await_piece(step, side, 1)
+                await_pieces(step, side, [0, 1])
             advance(step, rim, range(x_cuts[j][0], sum(x_cuts[j])))
             if step < 7:
-                for up in (0, 1):
-                    start(step + 1, ("gx", up), j)
+                for side in x_sides:
+                    start(step + 1, side, [j])
                 for side in edges:
-                    start(step + 1, side, 0)
-                    start(step + 1, side, 1)
-        await_piece(step, ("gy", 0), 2)
-        await_piece(step, ("gy", 1), 2)
-        advance(step, range(2, nx - 2), [0, 1, ny - 2, ny - 1])
-        if step < 7:
-            start(step + 1, ("gy", 0), 2)
-            start(step + 1, ("gy", 1), 2)
-        if step == 3:
-            start_density(1, 0)
-            start_density(1, 1)
+                    start(step + 1, side, [0, 1])
+            if n == min(1, chunks - 1):
+                for piece in (2, 3):
+                    for side in y_sides:
+                        await_pieces(step, side, [piece])
+                    advance(step, range(y_cuts[piece][0], sum(y_cuts[piece])), [0, 1, ny - 2, ny - 1])
+                    if step < 7:
+                        for side in y_sides:
+                            start(step + 1, side, [piece])
+                if step == 3:
+                    start_density(1, 0)
+                    start_density(1, 1)
         for x in range(2, nx - 2):
             advance(step, [x], range(2, ny - 2))
         if step == 3:
             start_density(1, 2)
 
-    for step in range(8):
-        for side in sides:
-
-            @pl.when(has[side])
-            def _():
-                for piece in range(chunks if side[0] == "gx" else 3):
+    for side in x_sides + y_sides:
+
+        def drain():
+            for step in range(8):
+                for piece in range(chunks if side[0] == "gx" else 4):
                     send_copy(step, side, piece).wait_send()
+
+        each(side, drain)
 
     for which in (0, 1):
         for j in range(n_b - 1):
@@ -281,7 +302,7 @@
             jax.ShapeDtypeStruct((nx, ny, nf, nz), jnp.float32),
             jax.ShapeDtypeStruct((ny, nx, nz), jnp.float32),
         ),
-        in_specs=[pl.BlockSpec(memory_space=pl.ANY)] * 2,
+        in_specs=[pl.BlockSpec(memory_space=pltpu.HBM)] * 2,
         out_specs=(pl.BlockSpec(memory_space=pltpu.VMEM),) * 2,
         scratch_shapes=[
             *[pltpu.VMEM((nx + 4, ny + 4, nf, nz), jnp.float32)] * 8,
@@ -292,8 +313,8 @@
             dma((2,)),
             dma((8, 2, 6)),
             dma((8, 2, 6)),
-            dma((8, 2, 3)),
-            dma((8, 2, 3)),
+            dma((8, 2, 4)),
+            dma((8, 2, 4)),
             dma((2, n_b - 1, 3)),
             dma((2, n_b - 1, 3)),
         ],

time: 41.4 us -> 40.7 us (0.983)
  Pallas kernels: 37.1 us -> 36.5 us
    pallas_call x1, Pallas kernels: 37.1 us -> 36.5 us  [body(): pl.pallas_call(functools.partial(kernel, counts), out_shape=(jax.ShapeDty...]
where the time goes in v4:
time: 40.7 us; the launch traced here: 40.5 us
  Pallas kernels  36.5 us (90%)
  local copies, waits for them, and re-layouts  3.38 us (8%)
  between operations  0.65 us (2%)
    pallas_call x1, Pallas kernels, body(): pl.pallas_call(functools.partial(kernel, counts), out_shape=(jax.ShapeDty...  36.5 us
    unnamed x6, local copies, waits for them, and re-layouts  3.38 us

profile of v4, /device:TPU:0, one launch (start us, length us, event | category | flops | bytes accessed | tf_op | source)
XLA Modules:
  0.0 40.5 jit_solution(6024102643655280447)
XLA Ops:
  0.6 0.0 copy-start
  0.6 1.0 %copy-done = f32[2,4,8,12,128]{4,2,3,1,0:T(8,128)S(1)} copy-done((f32[2,4,8,12,128]{4,2,3,1,0:T(8,128)S(1)}, f32[2,4,8,12,128]{4,2,3,1,0:T(8,128)}, u32[]{:S(2)}) %copy-start) | copy-done | bytes 393240
  1.6 0.0 copy-start.1
  1.6 0.8 %copy-done.1 = f32[8,12,128]{2,0,1:T(8,128)S(1)} copy-done((f32[8,12,128]{2,0,1:T(8,128)S(1)}, f32[8,12,128]{2,0,1:T(8,128)}, u32[]{:S(2)}) %copy-start.1) | copy-done | bytes 49176
  2.4 36.5 %shard_map.41 = (f32[8,12,8,128]{3,2,1,0:T(8,128)S(1)}, f32[12,8,128]{2,1,0:T(8,128)S(1)}) custom-call(f32[8,12,8,128]{3,2,1,0:T(8,128)S(1)} %bitcast.8, f32[12,8,128]{2,1,0:T(8,128)S(1)} %bitcast.10), custom_call_target="tpu_custom_call" | custom-call | tf_op jit(solution)/shard_map/pallas_call | solution.py:299
  38.9 1.0 %copy.4 = f32[2,4,8,12,128]{4,2,3,1,0:T(8,128)} copy(f32[2,4,8,12,128]{4,1,0,3,2:T(4,128)S(1)} %bitcast.9) | data formatting | bytes 786432
  39.9 0.6 %copy.6 = f32[8,12,128]{2,0,1:T(8,128)} copy(f32[8,12,128]{2,0,1:T(8,128)S(1)} %bitcast.11) | data formatting | bytes 98304
Async XLA Ops:
  0.6 1.0 %copy-start = (f32[2,4,8,12,128]{4,2,3,1,0:T(8,128)S(1)}, f32[2,4,8,12,128]{4,2,3,1,0:T(8,128)}, u32[]{:S(2)}) copy-start(f32[2,4,8,12,128]{4,2,3,1,0:T(8,128)} %param.2) | copy-start | bytes 1179652
  1.6 0.8 %copy-start.1 = (f32[8,12,128]{2,0,1:T(8,128)S(1)}, f32[8,12,128]{2,0,1:T(8,128)}, u32[]{:S(2)}) copy-start(f32[8,12,128]{2,0,1:T(8,128)} %param.3) | copy-start | bytes 147460
